TPU v7x, 1024 devices: a whole 4x4x32 slice. The times are simulated.
1024 devices in a mesh: space: 16 (over x, y), sub: 64 (over z, core).
Axes of the slice: x: 4, y: 4, z: 32, core: 2. Of those that a mesh axis runs over, the one named last changes fastest.
Arguments:
- positions: float32 [3, 16, 4096, 128], P(None, 'space', 'sub'), may hold values from 0 to 1.5
- masses: float32 [16, 4096, 128], P('space', 'sub'), may hold values from 0.1 to 1
- occupancy: int32 [16, 4096], P('space', 'sub'), may hold values from 1 to 128
- export_slots: int32 [16, 2048], P('space', 'sub'), may hold values from 0 to 63, as said below
- export_count: int32 [16, 64], P('space', 'sub'), may hold values from 16 to 32
- pair_list: int32 [2, 16, 4096], P(None, 'space', 'sub'), may hold values from 0 to 319, as said below
- pair_count: int32 [16, 64], P('space', 'sub'), may hold values from 16 to 64
Outputs:
- forces: float32 [3, 16, 4096, 128], P(None, 'space', 'sub')
Inputs may be any that keep to these rules, and one draw needn't show every extreme that they name: `export_slots`: the 32 entries of one device are distinct own-leaf indices. `pair_list`: row 0 is a target own leaf, below 64; row 1 is a source pool leaf, below 320, never equal to the target.
All inputs are finite; a program needn't handle non-finite values.
Results may differ from a plain program's by a relative error of at most 0.0003.
Values sent between devices are 32-bit elements; how exact they have to be, the bound alone decides.
A program may use at most 32 MiB of HBM per device.

v0:
```python
import jax
import jax.numpy as jnp
from jax import lax
from jax.sharding import PartitionSpec as P

OFFSETS = ((-1, -1), (-1, 0), (-1, 1), (0, -1), (0, 1), (1, -1), (1, 0), (1, 1))
SOFTEN = 0.05
PRECISE = lax.Precision.HIGHEST


def extended(cells, sides, width):
    for axis, dim in sides:
        count = lax.axis_size(axis)
        head = lax.slice_in_dim(cells, 0, width, axis=dim)
        tail = lax.slice_in_dim(cells, cells.shape[dim] - width, cells.shape[dim], axis=dim)
        cells = jnp.concatenate(
            [
                lax.ppermute(tail, axis, [(i, (i + 1) % count) for i in range(count)]),
                cells,
                lax.ppermute(head, axis, [((i + 1) % count, i) for i in range(count)]),
            ],
            axis=dim,
        )
    return cells


def pair_block(target_pos, target_mass, source_pos, source_mass):
    separation = source_pos[:, :, None, :] - target_pos[:, :, :, None]
    distance = jnp.sum(separation * separation, axis=0)
    falloff = jnp.maximum(1.0 - distance, 0.0)
    softened = distance + SOFTEN
    weight = (
        target_mass[:, :, None]
        * source_mass[:, None, :]
        * falloff
        * falloff
        / (softened * jnp.sqrt(softened))
    )
    row_total = jnp.sum(weight, axis=2)
    col_total = jnp.sum(weight, axis=1)
    on_target = (
        jnp.einsum("bij,cbj->cbi", weight, source_pos, precision=PRECISE)
        - target_pos * row_total[None]
    )
    on_source = (
        jnp.einsum("bij,cbi->cbj", weight, target_pos, precision=PRECISE)
        - source_pos * col_total[None]
    )
    return (on_target, on_source)


def local(positions, masses, occupancy, export_slots, export_count, pair_list, pair_count):
    leaves = masses.shape[1]
    slot_width = masses.shape[2]
    sent_total = export_slots.shape[1]
    pair_slots = pair_list.shape[2]
    own_pos = positions[:, 0]
    slot_index = lax.broadcasted_iota(jnp.int32, (leaves, slot_width), 1)
    own_mass = jnp.where(slot_index < occupancy[0][:, None], masses[0], 0.0)
    slots = export_slots[0]
    keep = (jnp.arange(sent_total, dtype=jnp.int32) < export_count[0, 0]).astype(jnp.float32)
    sent_pos = jnp.take(own_pos, slots, axis=1)
    sent_mass = jnp.take(own_mass, slots, axis=0) * keep[:, None]
    outgoing = jnp.concatenate([sent_pos, sent_mass[None]], axis=0)[None, None]
    arrived = extended(outgoing, (("space", 0), ("sub", 1)), 1)
    ghosts = jnp.stack(
        [arrived[1 + space_step, 1 + sub_step] for space_step, sub_step in OFFSETS], axis=1
    )
    ghosts = ghosts.reshape(4, 8 * sent_total, slot_width)
    pool_pos = jnp.concatenate([own_pos, ghosts[:3]], axis=1)
    pool_mass = jnp.concatenate([own_mass, ghosts[3]], axis=0)
    pool_size = pool_mass.shape[0]
    own_index = jnp.arange(leaves, dtype=jnp.int32)
    live = (jnp.arange(pair_slots, dtype=jnp.int32) < pair_count[0, 0]).astype(jnp.float32)
    targets = jnp.concatenate([own_index, pair_list[0, 0]])
    sources = jnp.concatenate([own_index, pair_list[1, 0]])
    target_scale = jnp.concatenate([jnp.ones((leaves,), jnp.float32), live])
    source_scale = jnp.concatenate([jnp.zeros((leaves,), jnp.float32), live])

    def one_block(indices):
        tgt_rows, src_rows = indices
        return pair_block(
            pool_pos[:, tgt_rows], pool_mass[tgt_rows], pool_pos[:, src_rows], pool_mass[src_rows]
        )

    on_target, on_source = lax.map(one_block, (targets.reshape(8, -1), sources.reshape(8, -1)))
    on_target = jnp.moveaxis(on_target, 0, 1).reshape(3, -1, slot_width)
    on_source = jnp.moveaxis(on_source, 0, 1).reshape(3, -1, slot_width)
    pool_index = jnp.arange(pool_size, dtype=jnp.int32)
    onto_target = (targets[:, None] == pool_index[None, :]).astype(jnp.float32) * target_scale[
        :, None
    ]
    onto_source = (sources[:, None] == pool_index[None, :]).astype(jnp.float32) * source_scale[
        :, None
    ]
    pool_force = jnp.einsum("np,cnl->cpl", onto_target, on_target, precision=PRECISE)
    pool_force = pool_force + jnp.einsum("np,cnl->cpl", onto_source, on_source, precision=PRECISE)
    own_force = pool_force[:, :leaves]
    ghost_force = pool_force[:, leaves:].reshape(3, 8, sent_total, slot_width)

    def column(sub_step):
        return jnp.stack(
            [ghost_force[:, OFFSETS.index((space_step, sub_step))] for space_step in (-1, 0, 1)]
        )

    passed = extended(jnp.stack([column(-1), column(1)]), (("sub", 0),), 1)
    through = passed[0] + passed[3]
    toward_lower = ghost_force[:, OFFSETS.index((-1, 0))] + through[0]
    toward_upper = ghost_force[:, OFFSETS.index((1, 0))] + through[2]
    crossed = extended(jnp.stack([toward_lower, toward_upper]), (("space", 0),), 1)
    returned = through[1] + crossed[0] + crossed[3]
    own_force = own_force.at[:, slots].add(returned)
    return own_force[:, None]


def solution(mesh):
    return jax.shard_map(
        local,
        mesh=mesh,
        in_specs=(
            P(None, "space", "sub", None),
            P("space", "sub", None),
            P("space", "sub"),
            P("space", "sub"),
            P("space", "sub"),
            P(None, "space", "sub"),
            P("space", "sub"),
        ),
        out_specs=P(None, "space", "sub", None),
        check_vma=False,
    )
```

profile of v0, /device:TPU:30, one launch (start us, length us, event | category | flops | bytes accessed | tf_op | source)
XLA Modules:
  0.0 119.0 jit_solution(9881016310897926208)
XLA Ops:
  2.0 1.0 copy.78
  2.9 0.8 bitcast_select_fusion
  5.3 14.7 %collective-permute-start = (f32[1,1,4,32,128]{4,2,3,1,0:T(4,128)S(1)}, f32[1,1,4,32,128]{4,2,3,1,0:T(4,128)S(1)}, u32[]{:S(2)}, u32[]{:S(2)}) collective-permute-start(f32[1,1,4,32,128]{4,2,3,1,0:T(4,128)S(1)} %maximum_bitcast_fusion.2), channel_id=1, source_target_pairs={{0,64},{64,128},{128,192},{192,256},{256,320},{320,384},{384,448},... | collective-permute-start | bytes 196616 | tf_op jit(solution)/shard_map/ppermute | solution.py:18
  19.9 1.9 %collective-permute-start.1 = (f32[1,1,4,32,128]{4,2,3,1,0:T(4,128)S(1)}, f32[1,1,4,32,128]{4,2,3,1,0:T(4,128)S(1)}, u32[]{:S(2)}, u32[]{:S(2)}) collective-permute-start(f32[1,1,4,32,128]{4,2,3,1,0:T(4,128)S(1)} %maximum_bitcast_fusion.2), channel_id=1, source_target_pairs={{64,0},{128,64},{192,128},{256,192},{320,256},{384,320},{448,384},... | collective-permute-start | bytes 196616 | tf_op jit(solution)/shard_map/ppermute | solution.py:20
  21.9 0.7 slice_bitcast_fusion.10
  23.5 5.9 %collective-permute-done.1 = f32[1,1,4,32,128]{4,2,3,1,0:T(4,128)S(1)} collective-permute-done((f32[1,1,4,32,128]{4,2,3,1,0:T(4,128)S(1)}, f32[1,1,4,32,128]{4,2,3,1,0:T(4,128)S(1)}, u32[]{:S(2)}, u32[]{:S(2)}) %collective-permute-start.1) | collective-permute-done | bytes 65568 | tf_op jit(solution)/shard_map/ppermute | solution.py:20
  29.6 2.9 %collective-permute-start.3 = (f32[3,1,4,32,128]{4,2,3,1,0:T(4,128)S(1)}, f32[3,1,4,32,128]{4,2,3,1,0:T(4,128)S(1)}, u32[]{:S(2)}, u32[]{:S(2)}) collective-permute-start(f32[3,1,4,32,128]{4,2,3,1,0:T(4,128)S(1)} %pad_maximum_fusion.1), channel_id=1, source_target_pairs={{1,0},{2,1},{3,2},{4,3},{5,4},{6,5},{7,6},{8,7},{9,8},{10,9},{11,1... | collective-permute-start | bytes 589832 | tf_op jit(solution)/shard_map/ppermute | solution.py:20
  32.5 3.2 %collective-permute-done.2 = f32[3,1,4,32,128]{4,2,3,1,0:T(4,128)S(1)} collective-permute-done((f32[3,1,4,32,128]{4,2,3,1,0:T(4,128)S(1)}, f32[3,1,4,32,128]{4,2,3,1,0:T(4,128)S(1)}, u32[]{:S(2)}, u32[]{:S(2)}) %collective-permute-start.2) | collective-permute-done | bytes 196640 | tf_op jit(solution)/shard_map/ppermute | solution.py:18
  36.2 57.9 %while.12 = (s32[]{:T(128)}, f32[8,3,16,128]{3,1,2,0:T(4,128)S(1)}, f32[8,3,16,128]{3,1,2,0:T(4,128)S(1)}, s32[8,16]{1,0:T(8,128)S(1)}, f32[3,320,128]{2,0,1:T(4...) while((s32[]{:T(128)}, f32[8,3,16,128]{3,1,2,0:T(4,128)S(1)}, ...), condition=%wide.region_4.5_spmd, body=%wide.region_0.4_spmd.sunk | while | flops 23615584 | bytes 5776097 | solution.py:86
  37.5 1.0 multiply_reduce_fusion.2
  39.7 1.1 fusion.61
  40.7 1.0 fusion.63
  41.7 1.8 %fusion.62 = f32[8,3,16,128]{3,1,2,0:T(4,128)S(1)} fusion(f32[8,3,16,128]{3,1,2,0:T(4,128)S(1)} %get-tuple-element.150, s32[]{:T(128)} %get-tuple-element.149, f32[16,128,128]{2,1,0:T(8,128)S(1)} %get-tuple-element.138, f32[16,128]{1,0:T(8,128)S(1)} %get-tuple-element.139, f32[16,3,128]{2,1,0:T(4,128)S(1)} %gather_fusion, ...), kind=kOutput, calls=%fused_computation.17.clone.1 | convolution fusion | flops 9449472 | bytes 1155076 | tf_op jit(solution)/shard_map/while/body/eval_jaxpr/bij,cbj->cbi/dot_general | solution.py:42
  44.7 1.0 multiply_reduce_fusion.2
  46.9 1.1 fusion.61
  48.0 1.0 fusion.63
  49.0 1.8 %fusion.62 = f32[8,3,16,128]{3,1,2,0:T(4,128)S(1)} fusion(f32[8,3,16,128]{3,1,2,0:T(4,128)S(1)} %get-tuple-element.150, s32[]{:T(128)} %get-tuple-element.149, f32[16,128,128]{2,1,0:T(8,128)S(1)} %get-tuple-element.138, f32[16,128]{1,0:T(8,128)S(1)} %get-tuple-element.139, f32[16,3,128]{2,1,0:T(4,128)S(1)} %gather_fusion, ...), kind=kOutput, calls=%fused_computation.17.clone.1 | convolution fusion | flops 9449472 | bytes 1155076 | tf_op jit(solution)/shard_map/while/body/eval_jaxpr/bij,cbj->cbi/dot_general | solution.py:42
  52.0 1.0 multiply_reduce_fusion.2
  54.1 1.1 fusion.61
  55.2 1.0 fusion.63
  56.2 1.8 %fusion.62 = f32[8,3,16,128]{3,1,2,0:T(4,128)S(1)} fusion(f32[8,3,16,128]{3,1,2,0:T(4,128)S(1)} %get-tuple-element.150, s32[]{:T(128)} %get-tuple-element.149, f32[16,128,128]{2,1,0:T(8,128)S(1)} %get-tuple-element.138, f32[16,128]{1,0:T(8,128)S(1)} %get-tuple-element.139, f32[16,3,128]{2,1,0:T(4,128)S(1)} %gather_fusion, ...), kind=kOutput, calls=%fused_computation.17.clone.1 | convolution fusion | flops 9449472 | bytes 1155076 | tf_op jit(solution)/shard_map/while/body/eval_jaxpr/bij,cbj->cbi/dot_general | solution.py:42
  59.2 1.0 multiply_reduce_fusion.2
  61.4 1.1 fusion.61
  62.5 1.0 fusion.63
  63.5 1.8 %fusion.62 = f32[8,3,16,128]{3,1,2,0:T(4,128)S(1)} fusion(f32[8,3,16,128]{3,1,2,0:T(4,128)S(1)} %get-tuple-element.150, s32[]{:T(128)} %get-tuple-element.149, f32[16,128,128]{2,1,0:T(8,128)S(1)} %get-tuple-element.138, f32[16,128]{1,0:T(8,128)S(1)} %get-tuple-element.139, f32[16,3,128]{2,1,0:T(4,128)S(1)} %gather_fusion, ...), kind=kOutput, calls=%fused_computation.17.clone.1 | convolution fusion | flops 9449472 | bytes 1155076 | tf_op jit(solution)/shard_map/while/body/eval_jaxpr/bij,cbj->cbi/dot_general | solution.py:42
  66.4 1.0 multiply_reduce_fusion.2
  68.6 1.1 fusion.61
  69.7 1.0 fusion.63
  70.7 1.8 %fusion.62 = f32[8,3,16,128]{3,1,2,0:T(4,128)S(1)} fusion(f32[8,3,16,128]{3,1,2,0:T(4,128)S(1)} %get-tuple-element.150, s32[]{:T(128)} %get-tuple-element.149, f32[16,128,128]{2,1,0:T(8,128)S(1)} %get-tuple-element.138, f32[16,128]{1,0:T(8,128)S(1)} %get-tuple-element.139, f32[16,3,128]{2,1,0:T(4,128)S(1)} %gather_fusion, ...), kind=kOutput, calls=%fused_computation.17.clone.1 | convolution fusion | flops 9449472 | bytes 1155076 | tf_op jit(solution)/shard_map/while/body/eval_jaxpr/bij,cbj->cbi/dot_general | solution.py:42
  73.7 1.0 multiply_reduce_fusion.2
  75.9 1.1 fusion.61
  76.9 1.0 fusion.63
  77.9 1.8 %fusion.62 = f32[8,3,16,128]{3,1,2,0:T(4,128)S(1)} fusion(f32[8,3,16,128]{3,1,2,0:T(4,128)S(1)} %get-tuple-element.150, s32[]{:T(128)} %get-tuple-element.149, f32[16,128,128]{2,1,0:T(8,128)S(1)} %get-tuple-element.138, f32[16,128]{1,0:T(8,128)S(1)} %get-tuple-element.139, f32[16,3,128]{2,1,0:T(4,128)S(1)} %gather_fusion, ...), kind=kOutput, calls=%fused_computation.17.clone.1 | convolution fusion | flops 9449472 | bytes 1155076 | tf_op jit(solution)/shard_map/while/body/eval_jaxpr/bij,cbj->cbi/dot_general | solution.py:42
  80.9 1.0 multiply_reduce_fusion.2
  83.1 1.1 fusion.61
  84.2 1.0 fusion.63
  85.2 1.8 %fusion.62 = f32[8,3,16,128]{3,1,2,0:T(4,128)S(1)} fusion(f32[8,3,16,128]{3,1,2,0:T(4,128)S(1)} %get-tuple-element.150, s32[]{:T(128)} %get-tuple-element.149, f32[16,128,128]{2,1,0:T(8,128)S(1)} %get-tuple-element.138, f32[16,128]{1,0:T(8,128)S(1)} %get-tuple-element.139, f32[16,3,128]{2,1,0:T(4,128)S(1)} %gather_fusion, ...), kind=kOutput, calls=%fused_computation.17.clone.1 | convolution fusion | flops 9449472 | bytes 1155076 | tf_op jit(solution)/shard_map/while/body/eval_jaxpr/bij,cbj->cbi/dot_general | solution.py:42
  88.2 1.0 multiply_reduce_fusion.2
  90.3 1.1 fusion.61
  91.4 1.0 fusion.63
  92.4 1.8 %fusion.62 = f32[8,3,16,128]{3,1,2,0:T(4,128)S(1)} fusion(f32[8,3,16,128]{3,1,2,0:T(4,128)S(1)} %get-tuple-element.150, s32[]{:T(128)} %get-tuple-element.149, f32[16,128,128]{2,1,0:T(8,128)S(1)} %get-tuple-element.138, f32[16,128]{1,0:T(8,128)S(1)} %get-tuple-element.139, f32[16,3,128]{2,1,0:T(4,128)S(1)} %gather_fusion, ...), kind=kOutput, calls=%fused_computation.17.clone.1 | convolution fusion | flops 9449472 | bytes 1155076 | tf_op jit(solution)/shard_map/while/body/eval_jaxpr/bij,cbj->cbi/dot_general | solution.py:42
  95.6 3.0 %collective-permute-start.5 = (f32[1,3,3,32,128]{4,2,3,1,0:T(4,128)S(1)}, f32[1,3,3,32,128]{4,2,3,1,0:T(4,128)S(1)}, u32[]{:S(2)}, u32[]{:S(2)}) collective-permute-start(f32[1,3,3,32,128]{4,2,3,1,0:T(4,128)S(1)} %maximum_bitcast_fusion.1), channel_id=1, source_target_pairs={{1,0},{2,1},{3,2},{4,3},{5,4},{6,5},{7,6},{8,7},{9,8},{10,9},{11,1... | collective-permute-start | bytes 442376 | tf_op jit(solution)/shard_map/ppermute | solution.py:20
  98.8 3.0 %collective-permute-done.5 = f32[1,3,3,32,128]{4,2,3,1,0:T(4,128)S(1)} collective-permute-done((f32[1,3,3,32,128]{4,2,3,1,0:T(4,128)S(1)}, f32[1,3,3,32,128]{4,2,3,1,0:T(4,128)S(1)}, u32[]{:S(2)}, u32[]{:S(2)}) %collective-permute-start.5) | collective-permute-done | bytes 147488 | tf_op jit(solution)/shard_map/ppermute | solution.py:20
  101.8 3.3 %collective-permute-done.4 = f32[1,3,3,32,128]{4,2,3,1,0:T(4,128)S(1)} collective-permute-done((f32[1,3,3,32,128]{4,2,3,1,0:T(4,128)S(1)}, f32[1,3,3,32,128]{4,2,3,1,0:T(4,128)S(1)}, u32[]{:S(2)}, u32[]{:S(2)}) %collective-permute-start.4) | collective-permute-done | bytes 147488 | tf_op jit(solution)/shard_map/ppermute | solution.py:18
  105.2 1.9 %collective-permute-start.6 = (f32[1,3,32,128]{3,1,2,0:T(4,128)S(1)}, f32[1,3,32,128]{3,1,2,0:T(4,128)S(1)}, u32[]{:S(2)}, u32[]{:S(2)}) collective-permute-start(f32[1,3,32,128]{3,1,2,0:T(4,128)S(1)} %get-tuple-element.74), channel_id=1, source_target_pairs={{0,64},{64,128},{128,192},{192,256},{256,320},{320,384},{384,448},... | collective-permute-start | bytes 147464 | tf_op jit(solution)/shard_map/ppermute | solution.py:18
  107.2 3.9 %collective-permute-start.7 = (f32[1,3,32,128]{3,1,2,0:T(4,128)S(1)}, f32[1,3,32,128]{3,1,2,0:T(4,128)S(1)}, u32[]{:S(2)}, u32[]{:S(2)}) collective-permute-start(f32[1,3,32,128]{3,1,2,0:T(4,128)S(1)} %get-tuple-element.75), channel_id=1, source_target_pairs={{64,0},{128,64},{192,128},{256,192},{320,256},{384,320},{448,384},... | collective-permute-start | bytes 147464 | tf_op jit(solution)/shard_map/ppermute | solution.py:20
  111.4 5.2 %collective-permute-done.7 = f32[1,3,32,128]{3,1,2,0:T(4,128)S(1)} collective-permute-done((f32[1,3,32,128]{3,1,2,0:T(4,128)S(1)}, f32[1,3,32,128]{3,1,2,0:T(4,128)S(1)}, u32[]{:S(2)}, u32[]{:S(2)}) %collective-permute-start.7) | collective-permute-done | bytes 49184 | tf_op jit(solution)/shard_map/ppermute | solution.py:20
  116.7 1.6 %scatter_fusion = f32[3,64,128]{2,0,1:T(4,128)S(1)} fusion(f32[3,64,128]{2,0,1:T(4,128)S(1)} %copy.51, s32[32]{0:T(128)S(1)} %fusion.39, f32[32,3,128]{2,1,0:T(4,128)S(1)} %fusion.31), kind=kCustom, calls=%fused_computation.6 | custom fusion | flops 12288 | bytes 147584 | tf_op jit(solution)/shard_map/scatter-add | solution.py:112
  (125 shorter events, 24.8 us)
Async XLA Ops:
  5.3 18.2 %collective-permute-start = (f32[1,1,4,32,128]{4,2,3,1,0:T(4,128)S(1)}, f32[1,1,4,32,128]{4,2,3,1,0:T(4,128)S(1)}, u32[]{:S(2)}, u32[]{:S(2)}) collective-permute-start(f32[1,1,4,32,128]{4,2,3,1,0:T(4,128)S(1)} %maximum_bitcast_fusion.2), channel_id=1, source_target_pairs={{0,64},{64,128},{128,192},{192,256},{256,320},{320,384},{384,448},... | collective-permute-start | bytes 196616 | tf_op jit(solution)/shard_map/ppermute | solution.py:18
  19.9 9.5 %collective-permute-start.1 = (f32[1,1,4,32,128]{4,2,3,1,0:T(4,128)S(1)}, f32[1,1,4,32,128]{4,2,3,1,0:T(4,128)S(1)}, u32[]{:S(2)}, u32[]{:S(2)}) collective-permute-start(f32[1,1,4,32,128]{4,2,3,1,0:T(4,128)S(1)} %maximum_bitcast_fusion.2), channel_id=1, source_target_pairs={{64,0},{128,64},{192,128},{256,192},{320,256},{384,320},{448,384},... | collective-permute-start | bytes 196616 | tf_op jit(solution)/shard_map/ppermute | solution.py:20
  29.5 6.3 %collective-permute-start.2 = (f32[3,1,4,32,128]{4,2,3,1,0:T(4,128)S(1)}, f32[3,1,4,32,128]{4,2,3,1,0:T(4,128)S(1)}, u32[]{:S(2)}, u32[]{:S(2)}) collective-permute-start(f32[3,1,4,32,128]{4,2,3,1,0:T(4,128)S(1)} %pad_maximum_fusion.1), channel_id=1, source_target_pairs={{0,1},{1,2},{2,3},{3,4},{4,5},{5,6},{6,7},{7,8},{8,9},{9,10},{10,1... | collective-permute-start | bytes 589832 | tf_op jit(solution)/shard_map/ppermute | solution.py:18
  29.6 6.2 %collective-permute-start.3 = (f32[3,1,4,32,128]{4,2,3,1,0:T(4,128)S(1)}, f32[3,1,4,32,128]{4,2,3,1,0:T(4,128)S(1)}, u32[]{:S(2)}, u32[]{:S(2)}) collective-permute-start(f32[3,1,4,32,128]{4,2,3,1,0:T(4,128)S(1)} %pad_maximum_fusion.1), channel_id=1, source_target_pairs={{1,0},{2,1},{3,2},{4,3},{5,4},{6,5},{7,6},{8,7},{9,8},{10,9},{11,1... | collective-permute-start | bytes 589832 | tf_op jit(solution)/shard_map/ppermute | solution.py:20
  95.6 6.2 %collective-permute-start.5 = (f32[1,3,3,32,128]{4,2,3,1,0:T(4,128)S(1)}, f32[1,3,3,32,128]{4,2,3,1,0:T(4,128)S(1)}, u32[]{:S(2)}, u32[]{:S(2)}) collective-permute-start(f32[1,3,3,32,128]{4,2,3,1,0:T(4,128)S(1)} %maximum_bitcast_fusion.1), channel_id=1, source_target_pairs={{1,0},{2,1},{3,2},{4,3},{5,4},{6,5},{7,6},{8,7},{9,8},{10,9},{11,1... | collective-permute-start | bytes 442376 | tf_op jit(solution)/shard_map/ppermute | solution.py:20
  98.8 6.3 %collective-permute-start.4 = (f32[1,3,3,32,128]{4,2,3,1,0:T(4,128)S(1)}, f32[1,3,3,32,128]{4,2,3,1,0:T(4,128)S(1)}, u32[]{:S(2)}, u32[]{:S(2)}) collective-permute-start(f32[1,3,3,32,128]{4,2,3,1,0:T(4,128)S(1)} %maximum_bitcast_fusion), channel_id=1, source_target_pairs={{0,1},{1,2},{2,3},{3,4},{4,5},{5,6},{6,7},{7,8},{8,9},{9,10},{10,1... | collective-permute-start | bytes 442376 | tf_op jit(solution)/shard_map/ppermute | solution.py:18
  105.2 6.2 %collective-permute-start.6 = (f32[1,3,32,128]{3,1,2,0:T(4,128)S(1)}, f32[1,3,32,128]{3,1,2,0:T(4,128)S(1)}, u32[]{:S(2)}, u32[]{:S(2)}) collective-permute-start(f32[1,3,32,128]{3,1,2,0:T(4,128)S(1)} %get-tuple-element.74), channel_id=1, source_target_pairs={{0,64},{64,128},{128,192},{192,256},{256,320},{320,384},{384,448},... | collective-permute-start | bytes 147464 | tf_op jit(solution)/shard_map/ppermute | solution.py:18
  107.2 9.5 %collective-permute-start.7 = (f32[1,3,32,128]{3,1,2,0:T(4,128)S(1)}, f32[1,3,32,128]{3,1,2,0:T(4,128)S(1)}, u32[]{:S(2)}, u32[]{:S(2)}) collective-permute-start(f32[1,3,32,128]{3,1,2,0:T(4,128)S(1)} %get-tuple-element.75), channel_id=1, source_target_pairs={{64,0},{128,64},{192,128},{256,192},{320,256},{384,320},{448,384},... | collective-permute-start | bytes 147464 | tf_op jit(solution)/shard_map/ppermute | solution.py:20
where the time goes:
time: 119 us
  starting transfers between devices  28.5 us (24%)
  matrix products  23.1 us (19%)
  local copies, waits for them, and re-layouts  22.8 us (19%)
  other arithmetic  21.8 us (18%)
  waiting for transfers between devices  20.9 us (18%)
  between operations  1.62 us (1%)
    ppermute x4, starting transfers between devices, extended(): lax.ppermute(tail, axis, [(i, (i + 1) % count) for i in range(count)])  16.6 us
    ppermute x4, waiting for transfers between devices, extended(): lax.ppermute(head, axis, [((i + 1) % count, i) for i in range(count)])  14.1 us
    dot_general x8, matrix products, pair_block(): jnp.einsum('bij,cbj->cbi', weight, source_pos, precision=PRECISE)  14 us
    ppermute x4, starting transfers between devices, extended(): lax.ppermute(head, axis, [((i + 1) % count, i) for i in range(count)])  11.8 us
    reduce_sum x8, other arithmetic, pair_block(): col_total = jnp.sum(weight, axis=1)  8.65 us
    reduce_sum x8, other arithmetic, pair_block(): distance = jnp.sum(separation * separation, axis=0)  8.3 us
    dot_general x8, matrix products, pair_block(): jnp.einsum('bij,cbi->cbj', weight, target_pos, precision=PRECISE)  7.91 us
    ppermute x4, waiting for transfers between devices, extended(): lax.ppermute(tail, axis, [(i, (i + 1) % count) for i in range(count)])  6.76 us
  transfers between devices with their start and end apart: 8, of which 6 were waited for; matrix products, arithmetic and copies ran while one was open for 1% of the time, Pallas kernels for 0%

commit v1 on v0

v1 whole, which is shorter than its diff:
```python
import functools

import jax
import jax.numpy as jnp
from jax import lax
from jax.experimental import pallas as pl
from jax.experimental.pallas import tpu as pltpu
from jax.sharding import PartitionSpec as P

OFFSETS = ((-1, -1), (-1, 0), (-1, 1), (0, -1), (0, 1), (1, -1), (1, 0), (1, 1))
SOFTEN = 0.05
CENTRE = 0.75
MESH = pl.DeviceIdType.MESH
F32 = jnp.float32
BF16 = jnp.bfloat16
UNROLL = 4


def split3(x):
    h = x.astype(BF16).astype(F32)
    rest = x - h
    m = rest.astype(BF16).astype(F32)
    return h, m, rest - m


def pieces(leaf):
    twice = jnp.concatenate([leaf, leaf], axis=0)
    row = lax.broadcasted_iota(jnp.int32, (8, 128), 0)
    low = row < 4
    last = (row == 3) | (row == 7)
    centred = jnp.where(last, 0.0, twice - CENTRE)
    return twice, centred, low, last, leaf[3:4, :]


def squared(centred, last):
    q = 0.5 * jnp.sum(centred * centred, axis=0, keepdims=True)
    return split3(jnp.where(last, q, centred))


def target_features(centred, low, last):
    h, m, l = squared(centred, last)
    h1 = jnp.where(last, 1.0, h)
    m1 = jnp.where(last, 1.0, m)
    rows = [jnp.where(low, h, m), jnp.where(low, l, h1), jnp.where(low, h1, m1), jnp.zeros_like(h)]
    return jnp.concatenate(rows, axis=0)


def source_features(centred, low, last):
    h, m, l = squared(centred, last)
    head = jnp.where(last, 1.0, -2.0 * h)
    rows = [
        head,
        jnp.where(low, head, jnp.where(last, h, -2.0 * m)),
        jnp.where(low, jnp.where(last, m, -2.0 * l), jnp.where(last, l, -2.0 * m)),
        jnp.zeros_like(h),
    ]
    return jnp.concatenate(rows, axis=0)


def moments(centred, low, last, mass):
    h, m, l = split3(jnp.where(last, 1.0, centred) * mass)
    return jnp.concatenate([jnp.where(low, h, m), jnp.where(low, l, 0.0)], axis=0).astype(BF16)


def weights(distance):
    falloff = jnp.maximum(1.0 - distance, 0.0)
    root = lax.rsqrt(distance + SOFTEN)
    scaled = falloff * root
    return scaled * scaled * root


def halves(w):
    hi = w.astype(BF16)
    return hi, (w - hi.astype(F32)).astype(BF16)


def force(total, centred, mass):
    both = total[0:8] + total[8:16]
    both = both + pltpu.roll(both, 4, 0)
    return mass * (both - centred * both[3:4, :])


def dot(a, b):
    return jnp.dot(a, b, preferred_element_type=F32)


def dot_t(a, b):
    return lax.dot_general(a, b, (((1,), (1,)), ((), ())), preferred_element_type=F32)


def pipeline(groups, first, second, bufs):
    first(0, bufs[0])

    def step(i, carry):
        first(2 * i + 1, bufs[1])
        second(2 * i, bufs[0])
        first(2 * i + 2, bufs[0])
        second(2 * i + 1, bufs[1])
        return carry

    lax.fori_loop(0, groups // 2 - 1, step, 0)
    first(groups - 1, bufs[1])
    second(groups - 2, bufs[0])
    second(groups - 1, bufs[1])


def kernel(
    shape,
    pos_hbm, mass_hbm, occ_hbm, slots_hbm, ecount_hbm, pairs_hbm, pcount_hbm,
    out_ref,
    pos_v, mass_v, occ_s, slots_s, ecount_s, pairs_s, pcount_s, slots_v, pairs_v,
    sent, pool, target_t, hi0, lo0, hi1, lo1, self_f, pair_f, ghost_f, returned, acc,
    in_sem, send_sem, recv_sem, send2_sem, recv2_sem,
):
    n_space, n_sub = shape
    leaves = pos_v.shape[1]
    g_total = sent.shape[0]
    pair_slots = pairs_v.shape[2]
    s = lax.axis_index("space")
    r = lax.axis_index("sub")

    def place(a, b):
        return (lax.rem(s + a + n_space, n_space), lax.rem(r + b + n_sub, n_sub))

    loads = [
        pltpu.make_async_copy(src, dst, in_sem.at[i])
        for i, (src, dst) in enumerate(
            [
                (pos_hbm.at[:, 0], pos_v),
                (mass_hbm.at[0], mass_v),
                (slots_hbm, slots_s),
                (occ_hbm, occ_s),
                (ecount_hbm, ecount_s),
                (pairs_hbm, pairs_s),
                (pcount_hbm, pcount_s),
                (slots_hbm, slots_v),
                (pairs_hbm, pairs_v),
            ]
        )
    ]
    for load in loads:
        load.start()
    barrier = pltpu.get_barrier_semaphore()
    for a, b in OFFSETS:
        pl.semaphore_signal(barrier, inc=1, device_id=place(a, b), device_id_type=MESH)
    for load in loads:
        load.wait()

    lane = lax.broadcasted_iota(jnp.int32, (1, 128), 1)
    exported = ecount_s[0, 0]

    def gather(i, carry):
        for j in range(4):
            g = i * 4 + j
            slot = slots_s[0, g]
            for c in range(3):
                sent[g, pl.ds(c, 1), :] = pos_v[c, pl.ds(slot, 1), :]
            live = jnp.where(g < exported, occ_s[0, slot], 0)
            sent[g, pl.ds(3, 1), :] = jnp.where(lane < live, mass_v[pl.ds(slot, 1), :], 0.0)
        return carry

    lax.fori_loop(0, g_total // 4, gather, 0)
    pl.semaphore_wait(barrier, len(OFFSETS))

    out_copies = []
    for k, (a, b) in enumerate(OFFSETS):
        copy = pltpu.make_async_remote_copy(
            src_ref=sent,
            dst_ref=pool.at[pl.ds(leaves + k * g_total, g_total)],
            send_sem=send_sem.at[k],
            recv_sem=recv_sem.at[k],
            device_id=place(-a, -b),
            device_id_type=MESH,
        )
        copy.start()
        out_copies.append(copy)

    def own(i, carry):
        for j in range(4):
            leaf = i * 4 + j
            for c in range(3):
                pool[leaf, pl.ds(c, 1), :] = pos_v[c, pl.ds(leaf, 1), :]
            pool[leaf, pl.ds(3, 1), :] = jnp.where(
                lane < occ_s[0, leaf], mass_v[pl.ds(leaf, 1), :], 0.0
            )
        return carry

    lax.fori_loop(0, leaves // 4, own, 0)

    def self_first(group, buf):
        hi, lo = buf
        for j in range(UNROLL):
            leaf = group * UNROLL + j
            _, centred, low, last, _ = pieces(pool[leaf])
            at = target_features(centred, low, last).T.astype(BF16)
            target_t[leaf] = at
            hi[j], lo[j] = halves(weights(dot(at, source_features(centred, low, last).astype(BF16))))

    def self_second(group, buf):
        hi, lo = buf
        for j in range(UNROLL):
            leaf = group * UNROLL + j
            _, centred, low, last, mass = pieces(pool[leaf])
            mom = moments(centred, low, last, mass)
            f = force(dot(mom, hi[j]) + dot(mom, lo[j]), centred, mass)
            for c in range(3):
                self_f[c, pl.ds(leaf, 1), :] = f[c : c + 1, :]

    bufs = ((hi0, lo0), (hi1, lo1))
    pipeline(leaves // UNROLL, self_first, self_second, bufs)

    for copy in out_copies:
        copy.wait_recv()

    def pair_first(group, buf):
        hi, lo = buf
        for j in range(UNROLL):
            p = group * UNROLL + j
            _, centred, low, last, _ = pieces(pool[pairs_s[1, 0, p]])
            src = source_features(centred, low, last).astype(BF16)
            hi[j], lo[j] = halves(weights(dot(target_t[pairs_s[0, 0, p]], src)))

    def pair_second(group, buf):
        hi, lo = buf
        for j in range(UNROLL):
            p = group * UNROLL + j
            _, t_centred, low, last, t_mass = pieces(pool[pairs_s[0, 0, p]])
            _, s_centred, low, last, s_mass = pieces(pool[pairs_s[1, 0, p]])
            t_mom = moments(t_centred, low, last, t_mass)
            s_mom = moments(s_centred, low, last, s_mass)
            on_target = force(dot_t(s_mom, hi[j]) + dot_t(s_mom, lo[j]), t_centred, t_mass)
            on_source = force(dot(t_mom, hi[j]) + dot(t_mom, lo[j]), s_centred, s_mass)
            for c in range(3):
                pair_f[c, pl.ds(p, 1), :] = on_target[c : c + 1, :]
                pair_f[c, pl.ds(pair_slots + p, 1), :] = on_source[c : c + 1, :]

    pipeline(pair_slots // UNROLL, pair_first, pair_second, bufs)

    key = jnp.concatenate([pairs_v[0], pairs_v[1]], axis=1)
    slot = lax.broadcasted_iota(jnp.int32, (1, 2 * pair_slots), 1)
    slot = jnp.where(slot < pair_slots, slot, slot - pair_slots)
    key = jnp.where(slot < pcount_s[0, 0], key, -1)
    split = [piece.astype(BF16) for piece in split3(jnp.concatenate([pair_f[0], pair_f[1], pair_f[2]], axis=1))]

    def scatter(start, rows):
        index = lax.broadcasted_iota(jnp.int32, (rows, 2 * pair_slots), 0) + start
        pick = jnp.where(index == key, 1.0, 0.0).astype(BF16)
        return dot(pick, split[0]) + dot(pick, split[1]) + dot(pick, split[2])

    ghosts = scatter(leaves, 8 * g_total)
    for k in range(8):
        for c in range(3):
            ghost_f[k, c] = ghosts[k * g_total : (k + 1) * g_total, c * 128 : (c + 1) * 128]
    back_copies = []
    for k, (a, b) in enumerate(OFFSETS):
        copy = pltpu.make_async_remote_copy(
            src_ref=ghost_f.at[k],
            dst_ref=returned.at[k],
            send_sem=send2_sem.at[k],
            recv_sem=recv2_sem.at[k],
            device_id=place(a, b),
            device_id_type=MESH,
        )
        copy.start()
        back_copies.append(copy)

    mine = scatter(0, leaves)
    for c in range(3):
        acc[c] = mine[:, c * 128 : (c + 1) * 128] + self_f[c]
    for copy in out_copies:
        copy.wait_send()
    pick = jnp.where(
        lax.broadcasted_iota(jnp.int32, (leaves, g_total), 0) == slots_v[...], 1.0, 0.0
    ).astype(BF16)
    for copy in back_copies:
        copy.wait_recv()
    for c in range(3):
        total = returned[0, c]
        for k in range(1, 8):
            total = total + returned[k, c]
        h, m, l = split3(total)
        out_ref[c, 0] = (
            acc[c]
            + dot(pick, h.astype(BF16))
            + dot(pick, m.astype(BF16))
            + dot(pick, l.astype(BF16))
        )
    for copy in back_copies:
        copy.wait_send()


def local(shape, positions, masses, occupancy, export_slots, export_count, pair_list, pair_count):
    leaves, width = masses.shape[1:]
    g_total = export_slots.shape[1]
    pair_slots = pair_list.shape[2]
    anywhere = pl.BlockSpec(memory_space=pl.ANY)
    return pl.pallas_call(
        functools.partial(kernel, shape),
        out_shape=jax.ShapeDtypeStruct(positions.shape, F32),
        in_specs=[anywhere] * 7,
        out_specs=pl.BlockSpec(memory_space=pltpu.VMEM),
        scratch_shapes=[
            pltpu.VMEM((3, leaves, width), F32),
            pltpu.VMEM((leaves, width), F32),
            pltpu.SMEM((1, leaves), jnp.int32),
            pltpu.SMEM((1, g_total), jnp.int32),
            pltpu.SMEM((1, 1), jnp.int32),
            pltpu.SMEM((2, 1, pair_slots), jnp.int32),
            pltpu.SMEM((1, 1), jnp.int32),
            pltpu.VMEM((1, g_total), jnp.int32),
            pltpu.VMEM((2, 1, pair_slots), jnp.int32),
            pltpu.VMEM((g_total, 4, width), F32),
            pltpu.VMEM((leaves + 8 * g_total, 4, width), F32),
            pltpu.VMEM((leaves, width, 32), BF16),
            pltpu.VMEM((UNROLL, width, width), BF16),
            pltpu.VMEM((UNROLL, width, width), BF16),
            pltpu.VMEM((UNROLL, width, width), BF16),
            pltpu.VMEM((UNROLL, width, width), BF16),
            pltpu.VMEM((3, leaves, width), F32),
            pltpu.VMEM((3, 2 * pair_slots, width), F32),
            pltpu.VMEM((8, 3, g_total, width), F32),
            pltpu.VMEM((8, 3, g_total, width), F32),
            pltpu.VMEM((3, leaves, width), F32),
            pltpu.SemaphoreType.DMA((9,)),
            pltpu.SemaphoreType.DMA((8,)),
            pltpu.SemaphoreType.DMA((8,)),
            pltpu.SemaphoreType.DMA((8,)),
            pltpu.SemaphoreType.DMA((8,)),
        ],
        compiler_params=pltpu.CompilerParams(collective_id=0, has_side_effects=True),
    )(positions, masses, occupancy, export_slots, export_count, pair_list, pair_count)


def solution(mesh):
    return jax.shard_map(
        functools.partial(local, (mesh.shape["space"], mesh.shape["sub"])),
        mesh=mesh,
        in_specs=(
            P(None, "space", "sub", None),
            P("space", "sub", None),
            P("space", "sub"),
            P("space", "sub"),
            P("space", "sub"),
            P(None, "space", "sub"),
            P("space", "sub"),
        ),
        out_specs=P(None, "space", "sub", None),
        check_vma=False,
    )
```

time: 119 us -> 44.3 us (0.37)
  the two profiles are of different devices: /device:TPU:30 before, /device:TPU:1 now
where the time goes in v1:
time: 44.3 us; the launch traced here: 44.1 us
  Pallas kernels  41.3 us (93%)
  local copies, waits for them, and re-layouts  1.54 us (3%)
  between operations  1.3 us (3%)
    pallas_call x1, Pallas kernels, local(): pl.pallas_call(functools.partial(kernel, shape), out_shape=jax.ShapeDtype...  41.3 us
    unnamed x1, local copies, waits for them, and re-layouts  1.54 us

profile of v1, /device:TPU:1, one launch (start us, length us, event | category | flops | bytes accessed | tf_op | source)
XLA Modules:
  0.0 44.1 jit_solution(16009627591743916751)
XLA Ops:
  1.3 41.3 %shard_map.73 = f32[3,1,64,128]{3,2,1,0:T(8,128)} custom-call(f32[3,1,64,128]{3,2,1,0:T(8,128)} %pos_hbm.1, f32[1,64,128]{2,1,0:T(8,128)} %mass_hbm.1, s32[1,64]{1,0:T(1,128)} %occ_hbm.1, s32[1,32]{1,0:T(1,128)} %slots_hbm.1, s32[1,1]{1,0:T(1,128)S(6)} %copy.9.ecount_hbm, s32[2,1,64]{2,1,0:T(1,128)} %pairs_hbm.1, s32[1,1]{1,0:T(1,128)S(6)} %copy.10.pcount_hbm), custom_call_target="tpu_custom_call" | custom-call | tf_op jit(solution)/shard_map/pallas_call | solution.py:297
  42.6 1.5 %copy.11 = f32[3,1,64,128]{3,2,1,0:T(8,128)} copy(f32[3,1,64,128]{3,2,1,0:T(8,128)} %shard_map.73) | data formatting | bytes 196608

commit v2 on v1

v2 whole, which is shorter than its diff:
```python
import functools

import jax
import jax.numpy as jnp
from jax import lax
from jax.experimental import pallas as pl
from jax.experimental.pallas import tpu as pltpu
from jax.sharding import PartitionSpec as P

OFFSETS = ((-1, -1), (-1, 0), (-1, 1), (0, -1), (0, 1), (1, -1), (1, 0), (1, 1))
SOFTEN = 0.05
CENTRE = 0.75
MESH = pl.DeviceIdType.MESH
F32 = jnp.float32
BF16 = jnp.bfloat16
UNROLL = 4


def split3(x):
    h = x.astype(BF16).astype(F32)
    rest = x - h
    m = rest.astype(BF16).astype(F32)
    return h, m, rest - m


def rows_of():
    row = lax.broadcasted_iota(jnp.int32, (8, 128), 0)
    return row < 4, (row == 3) | (row == 7)


def centre(leaf, last):
    return jnp.where(last, 0.0, jnp.concatenate([leaf, leaf], axis=0) - CENTRE)


def squared(centred, last, extra):
    q = 0.5 * jnp.sum(centred * centred, axis=0, keepdims=True) + extra
    return split3(jnp.where(last, q, centred))


def target_features(centred, low, last):
    h, m, l = squared(centred, last, 0.0)
    h1 = jnp.where(last, 1.0, h)
    m1 = jnp.where(last, 1.0, m)
    rows = [jnp.where(low, h, m), jnp.where(low, l, h1), jnp.where(low, h1, m1), jnp.zeros_like(h)]
    return jnp.concatenate(rows, axis=0).astype(BF16)


def source_features(centred, low, last):
    h, m, l = squared(centred, last, SOFTEN)
    head = jnp.where(last, 1.0, -2.0 * h)
    rows = [
        head,
        jnp.where(low, head, jnp.where(last, h, -2.0 * m)),
        jnp.where(low, jnp.where(last, m, -2.0 * l), jnp.where(last, l, -2.0 * m)),
        jnp.zeros_like(h),
    ]
    return jnp.concatenate(rows, axis=0).astype(BF16)


def moments(centred, low, last, mass):
    h, m, l = split3(jnp.where(last, 1.0, centred) * mass)
    return jnp.concatenate([jnp.where(low, h, m), jnp.where(low, l, 0.0)], axis=0).astype(BF16)


def weights(softened):
    falloff = jnp.maximum((1.0 + SOFTEN) - softened, 0.0)
    root = lax.rsqrt(softened)
    scaled = falloff * root
    return scaled * scaled * root


def force(total, centred, mass):
    both = total[0:8] + total[8:16]
    both = both + pltpu.roll(both, 4, 0)
    return mass * (both - centred * both[3:4, :])


def dot(a, b):
    return jnp.dot(a, b, preferred_element_type=F32)


def dot_t(a, b):
    return lax.dot_general(a, b, (((1,), (1,)), ((), ())), preferred_element_type=F32)


def both_weights(left, right, source_left, source_right, buf, j):
    lane = lax.broadcasted_iota(jnp.int32, left.shape, 1)
    target = jnp.where(lane < 32, left, right)
    zero = jnp.zeros_like(source_left)
    source = jnp.concatenate(
        [
            jnp.concatenate([source_left, zero], axis=1),
            jnp.concatenate([zero, source_right], axis=1),
        ],
        axis=0,
    )
    w = weights(dot(target, source))
    hi = w.astype(BF16)
    lo = (w - hi.astype(F32)).astype(BF16)
    for i in range(2):
        buf[j + i, :, 0:128] = hi[:, i * 128 : (i + 1) * 128]
        buf[j + i, :, 128:256] = lo[:, i * 128 : (i + 1) * 128]


def folded(total):
    return total[:, 0:128] + total[:, 128:256]


def pipeline(groups, first, second, bufs):
    first(0, bufs[0])

    def step(i, carry):
        first(2 * i + 1, bufs[1])
        second(2 * i, bufs[0])
        first(2 * i + 2, bufs[0])
        second(2 * i + 1, bufs[1])
        return carry

    lax.fori_loop(0, groups // 2 - 1, step, 0)
    first(groups - 1, bufs[1])
    second(groups - 2, bufs[0])
    second(groups - 1, bufs[1])


def slot_of(a, b):
    if a == 0:
        return 3 + (b + 1) // 2
    return b + 1 if a < 0 else b + 6


def kernel(
    shape,
    pos_hbm, mass_hbm, occ_hbm, slots_hbm, ecount_hbm, pairs_hbm, pcount_hbm,
    out_ref,
    pos_v, mass_v, occ_s, slots_s, ecount_s, pairs_s, pcount_s, slots_v, pairs_v,
    sent, pool, target_t, moment_o, buf0, buf1, self_f, pair_f, ghost_f, via, passed, returned, acc,
    in_sem, send_sem, recv_sem, send2_sem, recv2_sem,
):
    n_space, n_sub = shape
    leaves = pos_v.shape[1]
    g_total = sent.shape[0]
    pair_slots = pairs_v.shape[2]
    s = lax.axis_index("space")
    r = lax.axis_index("sub")
    inner = 1 - 2 * lax.rem(r, 2)
    outer = -inner

    def place(a, b):
        return (lax.rem(s + a + n_space, n_space), lax.rem(r + b + n_sub, n_sub))

    loads = [
        pltpu.make_async_copy(src, dst, in_sem.at[i])
        for i, (src, dst) in enumerate(
            [
                (slots_hbm, slots_s),
                (occ_hbm, occ_s),
                (ecount_hbm, ecount_s),
                (pos_hbm.at[:, 0], pos_v),
                (mass_hbm.at[0], mass_v),
                (pairs_hbm, pairs_s),
                (pcount_hbm, pcount_s),
                (slots_hbm, slots_v),
                (pairs_hbm, pairs_v),
            ]
        )
    ]
    for load in loads:
        load.start()
    barrier = pltpu.get_barrier_semaphore()
    for a, b in OFFSETS:
        pl.semaphore_signal(barrier, inc=1, device_id=place(a, b), device_id_type=MESH)
    for load in loads:
        load.wait()

    lane = lax.broadcasted_iota(jnp.int32, (1, 128), 1)
    exported = ecount_s[0, 0]

    def gather(i, carry):
        for j in range(8):
            g = i * 8 + j
            slot = slots_s[0, g]
            for c in range(3):
                sent[g, pl.ds(c, 1), :] = pos_v[c, pl.ds(slot, 1), :]
            live = jnp.where(g < exported, occ_s[0, slot], 0)
            sent[g, pl.ds(3, 1), :] = jnp.where(lane < live, mass_v[pl.ds(slot, 1), :], 0.0)
        return carry

    lax.fori_loop(0, g_total // 8, gather, 0)
    pl.semaphore_wait(barrier, len(OFFSETS))

    def remote(src, dst, send, recv, role, a, b):
        copy = pltpu.make_async_remote_copy(
            src_ref=src,
            dst_ref=dst,
            send_sem=send.at[role],
            recv_sem=recv.at[role],
            device_id=place(a, b),
            device_id_type=MESH,
        )
        copy.start()
        return copy

    def ghosts_at(slot):
        return pool.at[pl.ds(leaves + slot * g_total, g_total)]

    def export(role, a, b, slot, src=sent):
        return remote(src, ghosts_at(slot), send_sem, recv_sem, role, a, b)

    ahead = [export(0, 1, 0, slot_of(-1, 0)), export(1, -1, 0, slot_of(1, 0))]
    out_copies = [
        export(4, 1, outer, inner + 1),
        export(5, -1, outer, inner + 6),
        export(3, 0, outer, 3 + (inner + 1) // 2),
        export(2, 0, inner, 3 + (outer + 1) // 2),
    ]

    def own(i, carry):
        for j in range(8):
            leaf = i * 8 + j
            for c in range(3):
                pool[leaf, pl.ds(c, 1), :] = pos_v[c, pl.ds(leaf, 1), :]
            pool[leaf, pl.ds(3, 1), :] = jnp.where(
                lane < occ_s[0, leaf], mass_v[pl.ds(leaf, 1), :], 0.0
            )
        return carry

    lax.fori_loop(0, leaves // 8, own, 0)

    def self_first(group, buf):
        low, last = rows_of()
        for j in range(0, UNROLL, 2):
            targets, sources = [], []
            for leaf in (group * UNROLL + j, group * UNROLL + j + 1):
                centred = centre(pool[leaf], last)
                feature = target_features(centred, low, last)
                target = jnp.concatenate([feature, feature], axis=0).T
                target_t[leaf] = target
                targets.append(target)
                sources.append(source_features(centred, low, last))
            both_weights(*targets, *sources, buf, j)

    def self_second(group, buf):
        low, last = rows_of()
        for j in range(UNROLL):
            leaf = group * UNROLL + j
            block = pool[leaf]
            centred, mass = centre(block, last), block[3:4, :]
            mom = moments(centred, low, last, mass)
            moment_o[leaf] = mom
            f = force(folded(dot(mom, buf[j])), centred, mass)
            for c in range(3):
                self_f[c, pl.ds(leaf, 1), :] = f[c : c + 1, :]

    bufs = (buf0, buf1)
    pipeline(leaves // UNROLL, self_first, self_second, bufs)

    for role, copy in enumerate(ahead):
        copy.wait_recv()
        a = 2 * role - 1
        slot = slot_of(a, 0)
        out_copies.append(export(6 + role, 0, inner, (outer + 1) if a < 0 else (outer + 6), ghosts_at(slot)))
    for copy in out_copies:
        copy.wait_recv()

    def pair_first(group, buf):
        low, last = rows_of()
        for j in range(0, UNROLL, 2):
            targets, sources = [], []
            for p in (group * UNROLL + j, group * UNROLL + j + 1):
                targets.append(target_t[pairs_s[0, 0, p]])
                centred = centre(pool[pairs_s[1, 0, p]], last)
                sources.append(source_features(centred, low, last))
            both_weights(*targets, *sources, buf, j)

    def pair_second(group, buf):
        low, last = rows_of()
        for j in range(UNROLL):
            p = group * UNROLL + j
            target, source = pairs_s[0, 0, p], pairs_s[1, 0, p]
            t_block, s_block = pool[target], pool[source]
            t_centred, t_mass = centre(t_block, last), t_block[3:4, :]
            s_centred, s_mass = centre(s_block, last), s_block[3:4, :]
            s_mom = moments(s_centred, low, last, s_mass)
            s_mom = jnp.concatenate([s_mom, s_mom], axis=1)
            on_target = force(dot_t(s_mom, buf[j]), t_centred, t_mass)
            on_source = force(folded(dot(moment_o[target], buf[j])), s_centred, s_mass)
            for c in range(3):
                pair_f[c, pl.ds(p, 1), :] = on_target[c : c + 1, :]
                pair_f[c, pl.ds(pair_slots + p, 1), :] = on_source[c : c + 1, :]

    pipeline(pair_slots // UNROLL, pair_first, pair_second, bufs)

    key = jnp.concatenate([pairs_v[0], pairs_v[1]], axis=1)
    slot = lax.broadcasted_iota(jnp.int32, (1, 2 * pair_slots), 1)
    slot = jnp.where(slot < pair_slots, slot, slot - pair_slots)
    key = jnp.where(slot < pcount_s[0, 0], key, -1)
    key = jnp.concatenate([key, key], axis=1)

    def two(x):
        h = x.astype(BF16)
        return jnp.concatenate([h, (x - h.astype(F32)).astype(BF16)], axis=0)

    results = two(jnp.concatenate([pair_f[0], pair_f[1], pair_f[2]], axis=1))

    def scatter(starts, rows):
        index = lax.broadcasted_iota(jnp.int32, (rows, 4 * pair_slots), 0)
        pick = [jnp.where(index + start == key, 1.0, 0.0) for start in starts]
        return dot(jnp.concatenate(pick, axis=0).astype(BF16), results)

    order = [inner + 1, inner + 6, 3 + (inner + 1) // 2]
    order += [outer + 1, outer + 6, 3 + (outer + 1) // 2, slot_of(-1, 0), slot_of(1, 0)]
    ghosts = scatter([leaves + slot * g_total for slot in order], g_total)
    for k in range(8):
        for c in range(3):
            ghost_f[k, c] = ghosts[k * g_total : (k + 1) * g_total, c * 128 : (c + 1) * 128]

    def back(role, a, b, src, dst):
        return remote(src, dst, send2_sem, recv2_sem, role, a, b)

    vias = [back(0, 0, inner, ghost_f.at[0], via.at[0]), back(1, 0, inner, ghost_f.at[1], via.at[1])]
    returns = [
        back(3, -1, outer, ghost_f.at[3], returned.at[1]),
        back(4, 1, outer, ghost_f.at[4], returned.at[2]),
        back(5, 0, outer, ghost_f.at[5], returned.at[3]),
        back(2, 0, inner, ghost_f.at[2], returned.at[0]),
    ]
    for i, copy in enumerate(vias):
        copy.wait_recv()
        passed[i] = ghost_f[6 + i] + via[i]
        returns.append(back(6 + i, 2 * i - 1, 0, passed.at[i], returned.at[4 + i]))

    mine = scatter([0], leaves)
    for c in range(3):
        acc[c] = mine[:, c * 128 : (c + 1) * 128] + self_f[c]
    for copy in ahead + out_copies + vias:
        copy.wait_send()
    slots2 = jnp.concatenate([slots_v[...], slots_v[...]], axis=1)
    index = lax.broadcasted_iota(jnp.int32, (leaves, 2 * g_total), 0)
    pick = jnp.where(index == slots2, 1.0, 0.0).astype(BF16)
    for copy in returns:
        copy.wait_recv()
    for c in range(3):
        total = returned[0, c]
        for k in range(1, 6):
            total = total + returned[k, c]
        out_ref[c, 0] = acc[c] + dot(pick, two(total))
    for copy in returns:
        copy.wait_send()


def local(shape, positions, masses, occupancy, export_slots, export_count, pair_list, pair_count):
    leaves, width = masses.shape[1:]
    g_total = export_slots.shape[1]
    pair_slots = pair_list.shape[2]
    far = pl.BlockSpec(memory_space=pltpu.HBM)
    return pl.pallas_call(
        functools.partial(kernel, shape),
        out_shape=pltpu.VMEM(positions.shape, F32),
        in_specs=[far] * 7,
        out_specs=pl.BlockSpec(memory_space=pltpu.VMEM),
        scratch_shapes=[
            pltpu.VMEM((3, leaves, width), F32),
            pltpu.VMEM((leaves, width), F32),
            pltpu.SMEM((1, leaves), jnp.int32),
            pltpu.SMEM((1, g_total), jnp.int32),
            pltpu.SMEM((1, 1), jnp.int32),
            pltpu.SMEM((2, 1, pair_slots), jnp.int32),
            pltpu.SMEM((1, 1), jnp.int32),
            pltpu.VMEM((1, g_total), jnp.int32),
            pltpu.VMEM((2, 1, pair_slots), jnp.int32),
            pltpu.VMEM((g_total, 4, width), F32),
            pltpu.VMEM((leaves + 8 * g_total, 4, width), F32),
            pltpu.VMEM((leaves, width, 64), BF16),
            pltpu.VMEM((leaves, 16, width), BF16),
            pltpu.VMEM((UNROLL, width, 2 * width), BF16),
            pltpu.VMEM((UNROLL, width, 2 * width), BF16),
            pltpu.VMEM((3, leaves, width), F32),
            pltpu.VMEM((3, 2 * pair_slots, width), F32),
            pltpu.VMEM((8, 3, g_total, width), F32),
            pltpu.VMEM((2, 3, g_total, width), F32),
            pltpu.VMEM((2, 3, g_total, width), F32),
            pltpu.VMEM((6, 3, g_total, width), F32),
            pltpu.VMEM((3, leaves, width), F32),
            pltpu.SemaphoreType.DMA((9,)),
            pltpu.SemaphoreType.DMA((8,)),
            pltpu.SemaphoreType.DMA((8,)),
            pltpu.SemaphoreType.DMA((8,)),
            pltpu.SemaphoreType.DMA((8,)),
        ],
        compiler_params=pltpu.CompilerParams(collective_id=0, has_side_effects=True),
    )(positions, masses, occupancy, export_slots, export_count, pair_list, pair_count)


def solution(mesh):
    return jax.shard_map(
        functools.partial(local, (mesh.shape["space"], mesh.shape["sub"])),
        mesh=mesh,
        in_specs=(
            P(None, "space", "sub", None),
            P("space", "sub", None),
            P("space", "sub"),
            P("space", "sub"),
            P("space", "sub"),
            P(None, "space", "sub"),
            P("space", "sub"),
        ),
        out_specs=P(None, "space", "sub", None),
        check_vma=False,
    )
```

time: 44.3 us -> 40.5 us (0.914)
  Pallas kernels: 41.3 us -> 38.4 us
  local copies, waits for them, and re-layouts: 1.54 us -> 0.64 us
    pallas_call x1, Pallas kernels: 41.3 us -> 38.4 us  [local(): pl.pallas_call(functools.partial(kernel, shape), out_shape=pltpu.VMEM(pos...]
    unnamed x1, local copies, waits for them, and re-layouts: 1.54 us -> 0.64 us
where the time goes in v2:
time: 40.5 us; the launch traced here: 40.3 us
  Pallas kernels  38.4 us (95%)
  between operations  1.3 us (3%)
  local copies, waits for them, and re-layouts  0.64 us (2%)
    pallas_call x1, Pallas kernels, local(): pl.pallas_call(functools.partial(kernel, shape), out_shape=pltpu.VMEM(pos...  38.4 us

profile of v2, /device:TPU:1, one launch (start us, length us, event | category | flops | bytes accessed | tf_op | source)
XLA Modules:
  0.0 40.3 jit_solution(11407923708287342226)
XLA Ops:
  1.3 38.4 %shard_map.73 = f32[3,1,64,128]{3,2,1,0:T(8,128)S(1)} custom-call(f32[3,1,64,128]{3,2,1,0:T(8,128)} %pos_hbm.1, f32[1,64,128]{2,1,0:T(8,128)} %mass_hbm.1, s32[1,64]{1,0:T(1,128)} %occ_hbm.1, s32[1,32]{1,0:T(1,128)} %slots_hbm.1, s32[1,1]{1,0:T(1,128)S(6)} %copy.10.ecount_hbm, s32[2,1,64]{2,1,0:T(1,128)} %pairs_hbm.1, s32[1,1]{1,0:T(1,128)S(6)} %copy.11.pcount_hbm), custom_call_target="tpu_custom_call" | custom-call | tf_op jit(solution)/shard_map/pallas_call | solution.py:356
  39.7 0.6 %copy.9 = f32[3,1,64,128]{3,2,1,0:T(8,128)} copy(f32[3,1,64,128]{3,2,1,0:T(8,128)S(1)} %shard_map.73) | data formatting | bytes 196608

commit v3 on v2

--- a/solution.py
+++ b/solution.py
@@ -23,43 +23,63 @@
     return h, m, rest - m
 
 
-def rows_of():
+def masks():
     row = lax.broadcasted_iota(jnp.int32, (8, 128), 0)
     return row < 4, (row == 3) | (row == 7)
 
 
-def centre(leaf, last):
-    return jnp.where(last, 0.0, jnp.concatenate([leaf, leaf], axis=0) - CENTRE)
+def two_leaves(first, second, low, last):
+    both = jnp.concatenate([first, second], axis=0)
+    mass = jnp.where(low, both[3:4, :], both[7:8, :])
+    return jnp.where(last, 0.0, both - CENTRE), mass
+
+
+def swap(x):
+    return pltpu.roll(x, 4, 0)
 
 
 def squared(centred, last, extra):
-    q = 0.5 * jnp.sum(centred * centred, axis=0, keepdims=True) + extra
-    return split3(jnp.where(last, q, centred))
+    t = centred * centred
+    t = t + pltpu.roll(t, 1, 0)
+    t = t + pltpu.roll(t, 2, 0) + extra
+    return split3(jnp.where(last, t, centred))
+
+
+def halves(low, upper, lower):
+    return jnp.where(low, upper, swap(lower)), jnp.where(low, swap(upper), lower)
+
+
+def stacked(low, blocks):
+    parts = [halves(low, upper, lower) for upper, lower in blocks]
+    zero = jnp.zeros((8, 128), F32)
+    pad = [zero] * (4 - len(parts)) if len(parts) > 2 else []
+    return [jnp.concatenate([p[i] for p in parts] + pad, axis=0).astype(BF16) for i in range(2)]
 
 
 def target_features(centred, low, last):
     h, m, l = squared(centred, last, 0.0)
     h1 = jnp.where(last, 1.0, h)
     m1 = jnp.where(last, 1.0, m)
-    rows = [jnp.where(low, h, m), jnp.where(low, l, h1), jnp.where(low, h1, m1), jnp.zeros_like(h)]
-    return jnp.concatenate(rows, axis=0).astype(BF16)
+    return stacked(low, [(h, m), (l, h1), (h1, m1)])
 
 
 def source_features(centred, low, last):
     h, m, l = squared(centred, last, SOFTEN)
     head = jnp.where(last, 1.0, -2.0 * h)
-    rows = [
-        head,
-        jnp.where(low, head, jnp.where(last, h, -2.0 * m)),
-        jnp.where(low, jnp.where(last, m, -2.0 * l), jnp.where(last, l, -2.0 * m)),
-        jnp.zeros_like(h),
-    ]
-    return jnp.concatenate(rows, axis=0).astype(BF16)
-
-
-def moments(centred, low, last, mass):
+    minus = -2.0 * m
+    return stacked(
+        low,
+        [
+            (head, head),
+            (head, jnp.where(last, h, minus)),
+            (jnp.where(last, m, -2.0 * l), jnp.where(last, l, minus)),
+        ],
+    )
+
+
+def moments(centred, mass, low, last):
     h, m, l = split3(jnp.where(last, 1.0, centred) * mass)
-    return jnp.concatenate([jnp.where(low, h, m), jnp.where(low, l, 0.0)], axis=0).astype(BF16)
+    return stacked(low, [(h, m), (l, jnp.zeros_like(l))])
 
 
 def weights(softened):
@@ -69,57 +89,61 @@
     return scaled * scaled * root
 
 
-def force(total, centred, mass):
-    both = total[0:8] + total[8:16]
-    both = both + pltpu.roll(both, 4, 0)
-    return mass * (both - centred * both[3:4, :])
+def force(first, second, centred, mass, low):
+    a, b = (t[0:8, 0:128] + t[0:8, 128:256] + (t[8:16, 0:128] + t[8:16, 128:256]) for t in (first, second))
+    both = jnp.where(low, a, b) + swap(jnp.where(low, b, a))
+    return mass * (both - centred * jnp.where(low, both[3:4, :], both[7:8, :]))
 
 
 def dot(a, b):
     return jnp.dot(a, b, preferred_element_type=F32)
 
 
-def dot_t(a, b):
-    return lax.dot_general(a, b, (((1,), (1,)), ((), ())), preferred_element_type=F32)
-
-
-def both_weights(left, right, source_left, source_right, buf, j):
-    lane = lax.broadcasted_iota(jnp.int32, left.shape, 1)
-    target = jnp.where(lane < 32, left, right)
-    zero = jnp.zeros_like(source_left)
+def distances(targets, sources):
+    zero = jnp.zeros_like(sources[0])
     source = jnp.concatenate(
         [
-            jnp.concatenate([source_left, zero], axis=1),
-            jnp.concatenate([zero, source_right], axis=1),
+            jnp.concatenate([sources[0], zero], axis=1),
+            jnp.concatenate([zero, sources[1]], axis=1),
         ],
         axis=0,
     )
-    w = weights(dot(target, source))
-    hi = w.astype(BF16)
-    lo = (w - hi.astype(F32)).astype(BF16)
-    for i in range(2):
-        buf[j + i, :, 0:128] = hi[:, i * 128 : (i + 1) * 128]
-        buf[j + i, :, 128:256] = lo[:, i * 128 : (i + 1) * 128]
-
-
-def folded(total):
-    return total[:, 0:128] + total[:, 128:256]
-
-
-def pipeline(groups, first, second, bufs):
-    first(0, bufs[0])
+    return dot(jnp.concatenate(targets, axis=0).T, source)
+
+
+def weigh(dist, buf):
+    for j in range(UNROLL):
+        w = weights(dist[j])
+        buf[0, j] = w.astype(BF16)
+        buf[1, j] = (w - buf[0, j].astype(F32)).astype(BF16)
+
+
+def beside(buf, j):
+    return jnp.concatenate([buf[0, j], buf[1, j]], axis=1)
+
+
+def turned(buf, j):
+    return jnp.concatenate([buf[0, j].T, buf[1, j].T], axis=1)
+
+
+def pipeline(groups, measure, combine, dists, bufs):
+    measure(0, dists[0])
+    weigh(dists[0], bufs[0])
+    measure(1, dists[1])
 
     def step(i, carry):
-        first(2 * i + 1, bufs[1])
-        second(2 * i, bufs[0])
-        first(2 * i + 2, bufs[0])
-        second(2 * i + 1, bufs[1])
+        combine(2 * i, bufs[0])
+        weigh(dists[1], bufs[1])
+        measure(2 * i + 2, dists[0])
+        combine(2 * i + 1, bufs[1])
+        weigh(dists[0], bufs[0])
+        measure(2 * i + 3, dists[1])
         return carry
 
     lax.fori_loop(0, groups // 2 - 1, step, 0)
-    first(groups - 1, bufs[1])
-    second(groups - 2, bufs[0])
-    second(groups - 1, bufs[1])
+    combine(groups - 2, bufs[0])
+    weigh(dists[1], bufs[1])
+    combine(groups - 1, bufs[1])
 
 
 def slot_of(a, b):
@@ -133,7 +157,7 @@
     pos_hbm, mass_hbm, occ_hbm, slots_hbm, ecount_hbm, pairs_hbm, pcount_hbm,
     out_ref,
     pos_v, mass_v, occ_s, slots_s, ecount_s, pairs_s, pcount_s, slots_v, pairs_v,
-    sent, pool, target_t, moment_o, buf0, buf1, self_f, pair_f, ghost_f, via, passed, returned, acc,
+    sent, pool, target_o, moment_o, dist0, dist1, buf0, buf1, self_f, pair_f, ghost_f, via, passed, returned, acc,
     in_sem, send_sem, recv_sem, send2_sem, recv2_sem,
 ):
     n_space, n_sub = shape
@@ -155,10 +179,10 @@
                 (slots_hbm, slots_s),
                 (occ_hbm, occ_s),
                 (ecount_hbm, ecount_s),
+                (pcount_hbm, pcount_s),
                 (pos_hbm.at[:, 0], pos_v),
                 (mass_hbm.at[0], mass_v),
                 (pairs_hbm, pairs_s),
-                (pcount_hbm, pcount_s),
                 (slots_hbm, slots_v),
                 (pairs_hbm, pairs_v),
             ]
@@ -226,33 +250,32 @@
 
     lax.fori_loop(0, leaves // 8, own, 0)
 
-    def self_first(group, buf):
-        low, last = rows_of()
+    def rows_at(i):
+        return pl.ds(pl.multiple_of(8 * i, 8), 8)
+
+    def self_measure(group, dist):
+        low, last = masks()
         for j in range(0, UNROLL, 2):
-            targets, sources = [], []
-            for leaf in (group * UNROLL + j, group * UNROLL + j + 1):
-                centred = centre(pool[leaf], last)
-                feature = target_features(centred, low, last)
-                target = jnp.concatenate([feature, feature], axis=0).T
-                target_t[leaf] = target
-                targets.append(target)
-                sources.append(source_features(centred, low, last))
-            both_weights(*targets, *sources, buf, j)
-
-    def self_second(group, buf):
-        low, last = rows_of()
-        for j in range(UNROLL):
             leaf = group * UNROLL + j
-            block = pool[leaf]
-            centred, mass = centre(block, last), block[3:4, :]
-            mom = moments(centred, low, last, mass)
-            moment_o[leaf] = mom
-            f = force(folded(dot(mom, buf[j])), centred, mass)
-            for c in range(3):
-                self_f[c, pl.ds(leaf, 1), :] = f[c : c + 1, :]
-
-    bufs = (buf0, buf1)
-    pipeline(leaves // UNROLL, self_first, self_second, bufs)
+            centred, mass = two_leaves(pool[leaf], pool[leaf + 1], low, last)
+            targets = target_features(centred, low, last)
+            both = distances(targets, source_features(centred, low, last))
+            mom = moments(centred, mass, low, last)
+            for i in range(2):
+                dist[j + i] = both[:, i * 128 : (i + 1) * 128]
+                target_o[leaf + i] = targets[i]
+                moment_o[leaf + i] = mom[i]
+
+    def self_combine(group, buf):
+        low, last = masks()
+        for j in range(0, UNROLL, 2):
+            leaf = group * UNROLL + j
+            centred, mass = two_leaves(pool[leaf], pool[leaf + 1], low, last)
+            sums = [dot(moment_o[leaf + i], beside(buf, j + i)) for i in range(2)]
+            self_f[rows_at(group * (UNROLL // 2) + j // 2), :] = force(*sums, centred, mass, low)
+
+    stages = ((dist0, dist1), (buf0, buf1))
+    pipeline(leaves // UNROLL, self_measure, self_combine, *stages)
 
     for role, copy in enumerate(ahead):
         copy.wait_recv()
@@ -262,33 +285,31 @@
     for copy in out_copies:
         copy.wait_recv()
 
-    def pair_first(group, buf):
-        low, last = rows_of()
+    def pair_measure(group, dist):
+        low, last = masks()
         for j in range(0, UNROLL, 2):
-            targets, sources = [], []
-            for p in (group * UNROLL + j, group * UNROLL + j + 1):
-                targets.append(target_t[pairs_s[0, 0, p]])
-                centred = centre(pool[pairs_s[1, 0, p]], last)
-                sources.append(source_features(centred, low, last))
-            both_weights(*targets, *sources, buf, j)
-
-    def pair_second(group, buf):
-        low, last = rows_of()
-        for j in range(UNROLL):
             p = group * UNROLL + j
-            target, source = pairs_s[0, 0, p], pairs_s[1, 0, p]
-            t_block, s_block = pool[target], pool[source]
-            t_centred, t_mass = centre(t_block, last), t_block[3:4, :]
-            s_centred, s_mass = centre(s_block, last), s_block[3:4, :]
-            s_mom = moments(s_centred, low, last, s_mass)
-            s_mom = jnp.concatenate([s_mom, s_mom], axis=1)
-            on_target = force(dot_t(s_mom, buf[j]), t_centred, t_mass)
-            on_source = force(folded(dot(moment_o[target], buf[j])), s_centred, s_mass)
-            for c in range(3):
-                pair_f[c, pl.ds(p, 1), :] = on_target[c : c + 1, :]
-                pair_f[c, pl.ds(pair_slots + p, 1), :] = on_source[c : c + 1, :]
-
-    pipeline(pair_slots // UNROLL, pair_first, pair_second, bufs)
+            centred, mass = two_leaves(pool[pairs_s[1, 0, p]], pool[pairs_s[1, 0, p + 1]], low, last)
+            targets = [target_o[pairs_s[0, 0, p]], target_o[pairs_s[0, 0, p + 1]]]
+            both = distances(targets, source_features(centred, low, last))
+            for i in range(2):
+                dist[j + i] = both[:, i * 128 : (i + 1) * 128]
+
+    def pair_combine(group, buf):
+        low, last = masks()
+        for j in range(0, UNROLL, 2):
+            p = group * UNROLL + j
+            at = group * (UNROLL // 2) + j // 2
+            targets = [pairs_s[0, 0, p], pairs_s[0, 0, p + 1]]
+            t_centred, t_mass = two_leaves(*[pool[t] for t in targets], low, last)
+            centred, mass = two_leaves(pool[pairs_s[1, 0, p]], pool[pairs_s[1, 0, p + 1]], low, last)
+            mom = moments(centred, mass, low, last)
+            sums = [dot(moment_o[targets[i]], beside(buf, j + i)) for i in range(2)]
+            pair_f[rows_at(pair_slots // 2 + at), :] = force(*sums, centred, mass, low)
+            sums = [dot(mom[i], turned(buf, j + i)) for i in range(2)]
+            pair_f[rows_at(at), :] = force(*sums, t_centred, t_mass, low)
+
+    pipeline(pair_slots // UNROLL, pair_measure, pair_combine, *stages)
 
     key = jnp.concatenate([pairs_v[0], pairs_v[1]], axis=1)
     slot = lax.broadcasted_iota(jnp.int32, (1, 2 * pair_slots), 1)
@@ -300,7 +321,9 @@
         h = x.astype(BF16)
         return jnp.concatenate([h, (x - h.astype(F32)).astype(BF16)], axis=0)
 
-    results = two(jnp.concatenate([pair_f[0], pair_f[1], pair_f[2]], axis=1))
+    results = two(
+        jnp.concatenate([pair_f[pl.ds(c, 2 * pair_slots, stride=4), :] for c in range(3)], axis=1)
+    )
 
     def scatter(starts, rows):
         index = lax.broadcasted_iota(jnp.int32, (rows, 4 * pair_slots), 0)
@@ -331,7 +354,7 @@
 
     mine = scatter([0], leaves)
     for c in range(3):
-        acc[c] = mine[:, c * 128 : (c + 1) * 128] + self_f[c]
+        acc[c] = mine[:, c * 128 : (c + 1) * 128] + self_f[pl.ds(c, leaves, stride=4), :]
     for copy in ahead + out_copies + vias:
         copy.wait_send()
     slots2 = jnp.concatenate([slots_v[...], slots_v[...]], axis=1)
@@ -370,12 +393,14 @@
             pltpu.VMEM((2, 1, pair_slots), jnp.int32),
             pltpu.VMEM((g_total, 4, width), F32),
             pltpu.VMEM((leaves + 8 * g_total, 4, width), F32),
-            pltpu.VMEM((leaves, width, 64), BF16),
+            pltpu.VMEM((leaves, 32, width), BF16),
             pltpu.VMEM((leaves, 16, width), BF16),
-            pltpu.VMEM((UNROLL, width, 2 * width), BF16),
-            pltpu.VMEM((UNROLL, width, 2 * width), BF16),
-            pltpu.VMEM((3, leaves, width), F32),
-            pltpu.VMEM((3, 2 * pair_slots, width), F32),
+            pltpu.VMEM((UNROLL, width, width), F32),
+            pltpu.VMEM((UNROLL, width, width), F32),
+            pltpu.VMEM((2, UNROLL, width, width), BF16),
+            pltpu.VMEM((2, UNROLL, width, width), BF16),
+            pltpu.VMEM((4 * leaves, width), F32),
+            pltpu.VMEM((8 * pair_slots, width), F32),
             pltpu.VMEM((8, 3, g_total, width), F32),
             pltpu.VMEM((2, 3, g_total, width), F32),
             pltpu.VMEM((2, 3, g_total, width), F32),

time: 40.5 us -> 39.8 us (0.983)
  Pallas kernels: 38.4 us -> 37.7 us
    pallas_call x1, Pallas kernels: 38.4 us -> 37.7 us  [local(): pl.pallas_call(functools.partial(kernel, shape), out_shape=pltpu.VMEM(pos...]
where the time goes in v3:
time: 39.8 us; the launch traced here: 39.6 us
  Pallas kernels  37.7 us (95%)
  between operations  1.3 us (3%)
  local copies, waits for them, and re-layouts  0.64 us (2%)
    pallas_call x1, Pallas kernels, local(): pl.pallas_call(functools.partial(kernel, shape), out_shape=pltpu.VMEM(pos...  37.7 us

profile of v3, /device:TPU:1, one launch (start us, length us, event | category | flops | bytes accessed | tf_op | source)
XLA Modules:
  0.0 39.6 jit_solution(3060060101211525092)
XLA Ops:
  1.3 37.7 %shard_map.73 = f32[3,1,64,128]{3,2,1,0:T(8,128)S(1)} custom-call(f32[3,1,64,128]{3,2,1,0:T(8,128)} %pos_hbm.1, f32[1,64,128]{2,1,0:T(8,128)} %mass_hbm.1, s32[1,64]{1,0:T(1,128)} %occ_hbm.1, s32[1,32]{1,0:T(1,128)} %slots_hbm.1, s32[1,1]{1,0:T(1,128)S(6)} %copy.10.ecount_hbm, s32[2,1,64]{2,1,0:T(1,128)} %pairs_hbm.1, s32[1,1]{1,0:T(1,128)S(6)} %copy.11.pcount_hbm), custom_call_target="tpu_custom_call" | custom-call | tf_op jit(solution)/shard_map/pallas_call | solution.py:379
  39.0 0.6 %copy.9 = f32[3,1,64,128]{3,2,1,0:T(8,128)} copy(f32[3,1,64,128]{3,2,1,0:T(8,128)S(1)} %shard_map.73) | data formatting | bytes 196608

commit v4 on v3

--- a/solution.py
+++ b/solution.py
@@ -13,7 +13,7 @@
 MESH = pl.DeviceIdType.MESH
 F32 = jnp.float32
 BF16 = jnp.bfloat16
-UNROLL = 4
+UNROLL = 8
 
 
 def split3(x):

time: 39.8 us -> 39.4 us (0.990)
  Pallas kernels: 37.7 us -> 37.3 us
where the time goes in v4:
time: 39.4 us; the launch traced here: 39.3 us
  Pallas kernels  37.3 us (95%)
  between operations  1.3 us (3%)
  local copies, waits for them, and re-layouts  0.64 us (2%)
    pallas_call x1, Pallas kernels, local(): pl.pallas_call(functools.partial(kernel, shape), out_shape=pltpu.VMEM(pos...  37.3 us

profile of v4, /device:TPU:1, one launch (start us, length us, event | category | flops | bytes accessed | tf_op | source)
XLA Modules:
  0.0 39.3 jit_solution(8240953872510906629)
XLA Ops:
  1.3 37.3 %shard_map.73 = f32[3,1,64,128]{3,2,1,0:T(8,128)S(1)} custom-call(f32[3,1,64,128]{3,2,1,0:T(8,128)} %pos_hbm.1, f32[1,64,128]{2,1,0:T(8,128)} %mass_hbm.1, s32[1,64]{1,0:T(1,128)} %occ_hbm.1, s32[1,32]{1,0:T(1,128)} %slots_hbm.1, s32[1,1]{1,0:T(1,128)S(6)} %copy.10.ecount_hbm, s32[2,1,64]{2,1,0:T(1,128)} %pairs_hbm.1, s32[1,1]{1,0:T(1,128)S(6)} %copy.11.pcount_hbm), custom_call_target="tpu_custom_call" | custom-call | tf_op jit(solution)/shard_map/pallas_call | solution.py:379
  38.6 0.6 %copy.9 = f32[3,1,64,128]{3,2,1,0:T(8,128)} copy(f32[3,1,64,128]{3,2,1,0:T(8,128)S(1)} %shard_map.73) | data formatting | bytes 196608

commit v5 on v4

--- a/solution.py
+++ b/solution.py
@@ -157,7 +157,7 @@
     pos_hbm, mass_hbm, occ_hbm, slots_hbm, ecount_hbm, pairs_hbm, pcount_hbm,
     out_ref,
     pos_v, mass_v, occ_s, slots_s, ecount_s, pairs_s, pcount_s, slots_v, pairs_v,
-    sent, pool, target_o, moment_o, dist0, dist1, buf0, buf1, self_f, pair_f, ghost_f, via, passed, returned, acc,
+    sent, pool, target_o, moment_o, dist0, dist1, buf0, buf1, self_f, pair_f, ghost_f, via, passed, returned, acc, back_f, pick_v, pick_s,
     in_sem, send_sem, recv_sem, send2_sem, recv2_sem,
 ):
     n_space, n_sub = shape
@@ -282,6 +282,24 @@
         a = 2 * role - 1
         slot = slot_of(a, 0)
         out_copies.append(export(6 + role, 0, inner, (outer + 1) if a < 0 else (outer + 6), ghosts_at(slot)))
+    key = jnp.concatenate([pairs_v[0], pairs_v[1]], axis=1)
+    slot = lax.broadcasted_iota(jnp.int32, (1, 2 * pair_slots), 1)
+    slot = jnp.where(slot < pair_slots, slot, slot - pair_slots)
+    key = jnp.where(slot < pcount_s[0, 0], key, -1)
+    key = jnp.concatenate([key, key], axis=1)
+
+    order = [inner + 1, inner + 6, 3 + (inner + 1) // 2]
+    order += [outer + 1, outer + 6, 3 + (outer + 1) // 2, slot_of(-1, 0), slot_of(1, 0)]
+    index = lax.broadcasted_iota(jnp.int32, (g_total, 4 * pair_slots), 0)
+    for k, slot in enumerate(order):
+        pick = jnp.where(index + (leaves + slot * g_total) == key, 1.0, 0.0)
+        pick_v[k * g_total : (k + 1) * g_total, :] = pick.astype(BF16)
+    index = lax.broadcasted_iota(jnp.int32, (leaves, 4 * pair_slots), 0)
+    pick_v[8 * g_total :, :] = jnp.where(index == key, 1.0, 0.0).astype(BF16)
+    slots2 = jnp.concatenate([slots_v[...], slots_v[...]], axis=1)
+    index = lax.broadcasted_iota(jnp.int32, (leaves, 2 * g_total), 0)
+    pick_s[...] = jnp.where(index == slots2, 1.0, 0.0).astype(BF16)
+
     for copy in out_copies:
         copy.wait_recv()
 
@@ -311,12 +329,6 @@
 
     pipeline(pair_slots // UNROLL, pair_measure, pair_combine, *stages)
 
-    key = jnp.concatenate([pairs_v[0], pairs_v[1]], axis=1)
-    slot = lax.broadcasted_iota(jnp.int32, (1, 2 * pair_slots), 1)
-    slot = jnp.where(slot < pair_slots, slot, slot - pair_slots)
-    key = jnp.where(slot < pcount_s[0, 0], key, -1)
-    key = jnp.concatenate([key, key], axis=1)
-
     def two(x):
         h = x.astype(BF16)
         return jnp.concatenate([h, (x - h.astype(F32)).astype(BF16)], axis=0)
@@ -325,49 +337,70 @@
         jnp.concatenate([pair_f[pl.ds(c, 2 * pair_slots, stride=4), :] for c in range(3)], axis=1)
     )
 
-    def scatter(starts, rows):
-        index = lax.broadcasted_iota(jnp.int32, (rows, 4 * pair_slots), 0)
-        pick = [jnp.where(index + start == key, 1.0, 0.0) for start in starts]
-        return dot(jnp.concatenate(pick, axis=0).astype(BF16), results)
-
-    order = [inner + 1, inner + 6, 3 + (inner + 1) // 2]
-    order += [outer + 1, outer + 6, 3 + (outer + 1) // 2, slot_of(-1, 0), slot_of(1, 0)]
-    ghosts = scatter([leaves + slot * g_total for slot in order], g_total)
+    ghosts = dot(pick_v[0 : 8 * g_total, :], results)
     for k in range(8):
         for c in range(3):
             ghost_f[k, c] = ghosts[k * g_total : (k + 1) * g_total, c * 128 : (c + 1) * 128]
 
     def back(role, a, b, src, dst):
-        return remote(src, dst, send2_sem, recv2_sem, role, a, b)
-
-    vias = [back(0, 0, inner, ghost_f.at[0], via.at[0]), back(1, 0, inner, ghost_f.at[1], via.at[1])]
+        return pltpu.make_async_remote_copy(
+            src_ref=src,
+            dst_ref=dst,
+            send_sem=send2_sem.at[role],
+            recv_sem=recv2_sem.at[role],
+            device_id=place(a, b),
+            device_id_type=MESH,
+        )
+
+    vias = [back(i, 0, inner, ghost_f.at[i], via.at[i]) for i in range(2)]
+    across = [back(i, 2 * i - 1, inner, ghost_f.at[i], returned.at[6 + i]) for i in range(2)]
+    straight = [back(6 + i, 2 * i - 1, 0, ghost_f.at[6 + i], returned.at[4 + i]) for i in range(2)]
+    summed = [back(6 + i, 2 * i - 1, 0, passed.at[i], returned.at[4 + i]) for i in range(2)]
     returns = [
         back(3, -1, outer, ghost_f.at[3], returned.at[1]),
         back(4, 1, outer, ghost_f.at[4], returned.at[2]),
         back(5, 0, outer, ghost_f.at[5], returned.at[3]),
         back(2, 0, inner, ghost_f.at[2], returned.at[0]),
     ]
-    for i, copy in enumerate(vias):
-        copy.wait_recv()
-        passed[i] = ghost_f[6 + i] + via[i]
-        returns.append(back(6 + i, 2 * i - 1, 0, passed.at[i], returned.at[4 + i]))
-
-    mine = scatter([0], leaves)
+    second_core = inner < 0
+
+    @pl.when(second_core)
+    def _():
+        for copy in vias + returns + straight:
+            copy.start()
+
+    @pl.when(jnp.logical_not(second_core))
+    def _():
+        for copy in across + returns:
+            copy.start()
+        for i, copy in enumerate(vias):
+            copy.wait_recv()
+            passed[i] = ghost_f[6 + i] + via[i]
+            summed[i].start()
+
+    mine = dot(pick_v[8 * g_total :, :], results)
     for c in range(3):
         acc[c] = mine[:, c * 128 : (c + 1) * 128] + self_f[pl.ds(c, leaves, stride=4), :]
     for copy in ahead + out_copies + vias:
         copy.wait_send()
-    slots2 = jnp.concatenate([slots_v[...], slots_v[...]], axis=1)
-    index = lax.broadcasted_iota(jnp.int32, (leaves, 2 * g_total), 0)
-    pick = jnp.where(index == slots2, 1.0, 0.0).astype(BF16)
-    for copy in returns:
+    for copy in returns + straight:
         copy.wait_recv()
     for c in range(3):
         total = returned[0, c]
         for k in range(1, 6):
             total = total + returned[k, c]
-        out_ref[c, 0] = acc[c] + dot(pick, two(total))
-    for copy in returns:
+        back_f[c] = total
+
+    @pl.when(second_core)
+    def _():
+        for copy in across:
+            copy.wait_recv()
+        for c in range(3):
+            back_f[c] = back_f[c] + (returned[6, c] + returned[7, c])
+
+    for c in range(3):
+        out_ref[c, 0] = acc[c] + dot(pick_s[...], two(back_f[c]))
+    for copy in returns + straight:
         copy.wait_send()
 
 
@@ -404,8 +437,11 @@
             pltpu.VMEM((8, 3, g_total, width), F32),
             pltpu.VMEM((2, 3, g_total, width), F32),
             pltpu.VMEM((2, 3, g_total, width), F32),
-            pltpu.VMEM((6, 3, g_total, width), F32),
+            pltpu.VMEM((8, 3, g_total, width), F32),
             pltpu.VMEM((3, leaves, width), F32),
+            pltpu.VMEM((3, g_total, width), F32),
+            pltpu.VMEM((8 * g_total + leaves, 4 * pair_slots), BF16),
+            pltpu.VMEM((leaves, 2 * g_total), BF16),
             pltpu.SemaphoreType.DMA((9,)),
             pltpu.SemaphoreType.DMA((8,)),
             pltpu.SemaphoreType.DMA((8,)),

time: 39.4 us -> 39.2 us (level)
  no operation moved by 1% of the time
where the time goes in v5:
time: 39.2 us; the launch traced here: 39 us
  Pallas kernels  37.1 us (95%)
  between operations  1.3 us (3%)
  local copies, waits for them, and re-layouts  0.64 us (2%)
    pallas_call x1, Pallas kernels, local(): pl.pallas_call(functools.partial(kernel, shape), out_shape=pltpu.VMEM(pos...  37.1 us

profile of v5, /device:TPU:1, one launch (start us, length us, event | category | flops | bytes accessed | tf_op | source)
XLA Modules:
  0.0 39.0 jit_solution(14801612801075223123)
XLA Ops:
  1.3 37.1 %shard_map.73 = f32[3,1,64,128]{3,2,1,0:T(8,128)S(1)} custom-call(f32[3,1,64,128]{3,2,1,0:T(8,128)} %pos_hbm.1, f32[1,64,128]{2,1,0:T(8,128)} %mass_hbm.1, s32[1,64]{1,0:T(1,128)} %occ_hbm.1, s32[1,32]{1,0:T(1,128)} %slots_hbm.1, s32[1,1]{1,0:T(1,128)S(6)} %copy.10.ecount_hbm, s32[2,1,64]{2,1,0:T(1,128)} %pairs_hbm.1, s32[1,1]{1,0:T(1,128)S(6)} %copy.11.pcount_hbm), custom_call_target="tpu_custom_call" | custom-call | tf_op jit(solution)/shard_map/pallas_call | solution.py:412
  38.4 0.6 %copy.9 = f32[3,1,64,128]{3,2,1,0:T(8,128)} copy(f32[3,1,64,128]{3,2,1,0:T(8,128)S(1)} %shard_map.73) | data formatting | bytes 196608

commit v6 on v5

--- a/solution.py
+++ b/solution.py
@@ -126,7 +126,7 @@
     return jnp.concatenate([buf[0, j].T, buf[1, j].T], axis=1)
 
 
-def pipeline(groups, measure, combine, dists, bufs):
+def pipeline(groups, measure, combine, dists, bufs, unroll=False):
     measure(0, dists[0])
     weigh(dists[0], bufs[0])
     measure(1, dists[1])
@@ -140,7 +140,11 @@
         measure(2 * i + 3, dists[1])
         return carry
 
-    lax.fori_loop(0, groups // 2 - 1, step, 0)
+    if unroll:
+        for i in range(groups // 2 - 1):
+            step(i, 0)
+    else:
+        lax.fori_loop(0, groups // 2 - 1, step, 0)
     combine(groups - 2, bufs[0])
     weigh(dists[1], bufs[1])
     combine(groups - 1, bufs[1])
@@ -251,7 +255,7 @@
     lax.fori_loop(0, leaves // 8, own, 0)
 
     def rows_at(i):
-        return pl.ds(pl.multiple_of(8 * i, 8), 8)
+        return pl.ds(8 * i if isinstance(i, int) else pl.multiple_of(8 * i, 8), 8)
 
     def self_measure(group, dist):
         low, last = masks()
@@ -327,7 +331,7 @@
             sums = [dot(mom[i], turned(buf, j + i)) for i in range(2)]
             pair_f[rows_at(at), :] = force(*sums, t_centred, t_mass, low)
 
-    pipeline(pair_slots // UNROLL, pair_measure, pair_combine, *stages)
+    pipeline(pair_slots // UNROLL, pair_measure, pair_combine, *stages, unroll=True)
 
     def two(x):
         h = x.astype(BF16)

time: 39.2 us -> 39 us (level)
  no operation moved by 1% of the time
where the time goes in v6:
time: 39 us; the launch traced here: 38.8 us
  Pallas kernels  36.9 us (95%)
  between operations  1.3 us (3%)
  local copies, waits for them, and re-layouts  0.64 us (2%)
    pallas_call x1, Pallas kernels, local(): pl.pallas_call(functools.partial(kernel, shape), out_shape=pltpu.VMEM(pos...  36.9 us

profile of v6, /device:TPU:1, one launch (start us, length us, event | category | flops | bytes accessed | tf_op | source)
XLA Modules:
  0.0 38.8 jit_solution(12777261851643536398)
XLA Ops:
  1.3 36.9 %shard_map.73 = f32[3,1,64,128]{3,2,1,0:T(8,128)S(1)} custom-call(f32[3,1,64,128]{3,2,1,0:T(8,128)} %pos_hbm.1, f32[1,64,128]{2,1,0:T(8,128)} %mass_hbm.1, s32[1,64]{1,0:T(1,128)} %occ_hbm.1, s32[1,32]{1,0:T(1,128)} %slots_hbm.1, s32[1,1]{1,0:T(1,128)S(6)} %copy.10.ecount_hbm, s32[2,1,64]{2,1,0:T(1,128)} %pairs_hbm.1, s32[1,1]{1,0:T(1,128)S(6)} %copy.11.pcount_hbm), custom_call_target="tpu_custom_call" | custom-call | tf_op jit(solution)/shard_map/pallas_call | solution.py:416
  38.2 0.6 %copy.9 = f32[3,1,64,128]{3,2,1,0:T(8,128)} copy(f32[3,1,64,128]{3,2,1,0:T(8,128)S(1)} %shard_map.73) | data formatting | bytes 196608

commit v7 on v6

--- a/solution.py
+++ b/solution.py
@@ -387,13 +387,14 @@
         acc[c] = mine[:, c * 128 : (c + 1) * 128] + self_f[pl.ds(c, leaves, stride=4), :]
     for copy in ahead + out_copies + vias:
         copy.wait_send()
-    for copy in returns + straight:
+    for copy in returns:
         copy.wait_recv()
     for c in range(3):
-        total = returned[0, c]
-        for k in range(1, 6):
-            total = total + returned[k, c]
-        back_f[c] = total
+        back_f[c] = (returned[0, c] + returned[1, c]) + (returned[2, c] + returned[3, c])
+    for copy in straight:
+        copy.wait_recv()
+    for c in range(3):
+        back_f[c] = back_f[c] + (returned[4, c] + returned[5, c])
 
     @pl.when(second_core)
     def _():

time: 39 us -> 39 us (level)
  no operation moved by 1% of the time
where the time goes in v7:
time: 39 us; the launch traced here: 38.8 us
  Pallas kernels  36.9 us (95%)
  between operations  1.3 us (3%)
  local copies, waits for them, and re-layouts  0.64 us (2%)
    pallas_call x1, Pallas kernels, local(): pl.pallas_call(functools.partial(kernel, shape), out_shape=pltpu.VMEM(pos...  36.9 us

profile of v7, /device:TPU:1, one launch (start us, length us, event | category | flops | bytes accessed | tf_op | source)
XLA Modules:
  0.0 38.8 jit_solution(9088499583204717771)
XLA Ops:
  1.3 36.9 %shard_map.73 = f32[3,1,64,128]{3,2,1,0:T(8,128)S(1)} custom-call(f32[3,1,64,128]{3,2,1,0:T(8,128)} %pos_hbm.1, f32[1,64,128]{2,1,0:T(8,128)} %mass_hbm.1, s32[1,64]{1,0:T(1,128)} %occ_hbm.1, s32[1,32]{1,0:T(1,128)} %slots_hbm.1, s32[1,1]{1,0:T(1,128)S(6)} %copy.10.ecount_hbm, s32[2,1,64]{2,1,0:T(1,128)} %pairs_hbm.1, s32[1,1]{1,0:T(1,128)S(6)} %copy.11.pcount_hbm), custom_call_target="tpu_custom_call" | custom-call | tf_op jit(solution)/shard_map/pallas_call | solution.py:417
  38.2 0.6 %copy.9 = f32[3,1,64,128]{3,2,1,0:T(8,128)} copy(f32[3,1,64,128]{3,2,1,0:T(8,128)S(1)} %shard_map.73) | data formatting | bytes 196608
